TPU v7x, 32 devices: a whole 2x2x4 slice. The times are simulated.
32 devices in a mesh: section: 4 (over z), tp: 2 (over y), dp: 4 (over x, core).
Axes of the slice: x: 2, y: 2, z: 4, core: 2. Of those that a mesh axis runs over, the one named last changes fastest.
Arguments:
- incoming: bfloat16 [4, 8, 128, 2304], P('section', ('dp', 'tp')), parts along dimension 1, may hold values from -6 to 6
- fresh_rows: bfloat16 [6, 8, 128, 2304], P(None, ('dp', 'tp')), parts along dimension 1, may hold values from -6 to 6
- entry_order: int32 [24], P('dp'), parts along dimension 0, may hold values from 0 to 5, each once
- flight_lengths: int32 [4, 8], P('section', 'dp'), parts along dimension 1, may hold values from 16 to 128
- pre_gain: float32 [4, 2304], P('section'), may hold values from 0.1 to 1.9
- post_gain: float32 [4, 2304], P('section'), may hold values from 0.1 to 1.9
- w_query: bfloat16 [4, 2304, 2048], P('section', None, 'tp'), may hold values from -0.125 to 0.125
- key_weight: bfloat16 [4, 2304, 1024], P('section', None, 'tp'), may hold values from -0.125 to 0.125
- value_weight: bfloat16 [4, 2304, 1024], P('section', None, 'tp'), may hold values from -0.125 to 0.125
- w_out: bfloat16 [4, 2048, 2304], P('section', 'tp'), may hold values from -0.125 to 0.125
Outputs:
- produced: bfloat16 [4, 8, 128, 2304], P('section', ('dp', 'tp')), parts along dimension 1
- advanced: bfloat16 [4, 8, 128, 2304], P('section', ('dp', 'tp')), parts along dimension 1
There are 4 independent parts, one for each index of `dp`. A program takes and returns all parts, laid end to end along the dimension named above; an argument that names none is the same for every part. Nothing has to cross between parts.
Inputs may be any that keep to these rules, and one draw needn't show every extreme that they name: `entry_order`: each waiting microbatch appears once.
All inputs are finite; a program needn't handle non-finite values.
Results may differ from a plain program's by a relative error of at most 0.012.
Values may be sent and summed in bfloat16 or wider, within the bound.
No kernel may reach another device: no remote copies, remote signals or barrier semaphores. Data moves between devices by JAX's collectives and lax.ppermute only.
A program may use at most 64 MiB of HBM per device.

v0:
```python
import jax
import jax.numpy as jnp
from jax import lax
from jax.sharding import PartitionSpec as P

HEAD_WIDTH = 128


EPSILON = 1e-06
SOFT_CAP = 50.0
QUERY_SCALE = 144.0 ** (-0.5)


def shifted(block, axis, distance):
    devices = range(lax.axis_size(axis))
    route = [(i - distance, i) for i in devices if i - distance in devices]
    return lax.ppermute(block, axis, route)


def normalize(values, gain):
    return values * lax.rsqrt(jnp.mean(values * values, -1, keepdims=True) + EPSILON) * gain


def apply_rotary(values, token_positions):
    half = values.shape[-1] // 2
    freq = 10000.0 ** (-2.0 * jnp.arange(half).astype(jnp.float32) / values.shape[-1])
    angle = token_positions[:, None].astype(jnp.float32) * freq[None, :]
    cosine = jnp.cos(angle)[:, None, :]
    sine = jnp.sin(angle)[:, None, :]
    first = values[..., :half]
    second = values[..., half:]
    return jnp.concatenate([first * cosine - second * sine, second * cosine + first * sine], -1)


def layer(held, lengths, gain_before, gain_after, w_query, key_weight, value_weight, w_out):
    seq_len = held.shape[1]
    width = held.shape[2]
    own_rows = held.shape[0] * seq_len
    flat = held.reshape(own_rows, width)
    widened = flat.astype(jnp.float32)
    local_query = w_query.shape[1] // HEAD_WIDTH
    local_kv = key_weight.shape[1] // HEAD_WIDTH
    query_cols = local_query * HEAD_WIDTH
    kv_cols = local_kv * HEAD_WIDTH
    normed_own = normalize(widened, gain_before).astype(jnp.bfloat16)
    normalized_input = lax.all_gather(normed_own, "tp", axis=0, tiled=True)
    count = normalized_input.shape[0]
    token_positions = jnp.arange(count) % seq_len
    query_matrix = jnp.dot(normalized_input, w_query, preferred_element_type=jnp.float32).reshape(
        count, local_query, HEAD_WIDTH
    )
    projected_keys = jnp.dot(
        normalized_input, key_weight, preferred_element_type=jnp.float32
    ).reshape(count, local_kv, HEAD_WIDTH)
    projected_values = jnp.dot(normalized_input, value_weight, preferred_element_type=jnp.float32)
    projected = jnp.concatenate(
        [
            apply_rotary(query_matrix, token_positions).reshape(count, query_cols),
            apply_rotary(projected_keys, token_positions).reshape(count, kv_cols),
            projected_values,
        ],
        1,
    ).astype(jnp.bfloat16)
    total_rows = projected.shape[0]
    batch = total_rows // seq_len
    group = local_query // local_kv
    query_matrix = projected[:, :query_cols].reshape(batch, seq_len, local_kv, group, HEAD_WIDTH)
    projected_keys = projected[:, query_cols : query_cols + kv_cols].reshape(
        batch, seq_len, local_kv, HEAD_WIDTH
    )
    projected_values = projected[:, query_cols + kv_cols :].reshape(
        batch, seq_len, local_kv, HEAD_WIDTH
    )
    scores = (
        jnp.einsum(
            "bqkgd,bskd->bkgqs", query_matrix, projected_keys, preferred_element_type=jnp.float32
        )
        * QUERY_SCALE
    )
    capped = SOFT_CAP * jnp.tanh(scores / SOFT_CAP)
    position = jnp.arange(seq_len)
    causal = position[None, :] <= position[:, None]
    allowed = causal[None, :, :] & (position[None, None, :] < lengths[:, None, None])
    raised = jnp.where(allowed[:, None, None, :, :], jnp.exp(capped), jnp.float32(0.0))
    probs = (raised / jnp.sum(raised, -1, keepdims=True)).astype(jnp.bfloat16)
    mixed = jnp.einsum(
        "bkgqs,bskd->bqkgd", probs, projected_values, preferred_element_type=jnp.float32
    ).astype(jnp.bfloat16)
    mixed_flat = mixed.reshape(total_rows, query_cols)
    branch_sum = lax.psum_scatter(
        jnp.dot(mixed_flat, w_out, preferred_element_type=jnp.float32).astype(jnp.bfloat16),
        "tp",
        scatter_dimension=0,
        tiled=True,
    ).astype(jnp.float32)
    return (widened + normalize(branch_sum, gain_after)).astype(jnp.bfloat16).reshape(held.shape)


def shards(
    incoming,
    fresh_rows,
    entry_order,
    flight_lengths,
    pre_gain,
    post_gain,
    w_query,
    key_weight,
    value_weight,
    w_out,
):
    section_index = lax.axis_index("section")
    produced = layer(
        incoming[0],
        flight_lengths[0],
        pre_gain[0],
        post_gain[0],
        w_query[0],
        key_weight[0],
        value_weight[0],
        w_out[0],
    )
    received = shifted(produced, "section", 1)
    entering = lax.dynamic_index_in_dim(fresh_rows, entry_order[0], 0, keepdims=False)
    advanced = jnp.where(section_index == 0, entering, received)
    return (produced[None], advanced[None])


def solution(mesh):
    in_specs = (
        P("section", ("dp", "tp"), None, None),
        P(None, ("dp", "tp"), None, None),
        P("dp"),
        P("section", "dp"),
        P("section", None),
        P("section", None),
        P("section", None, "tp"),
        P("section", None, "tp"),
        P("section", None, "tp"),
        P("section", "tp", None),
    )
    out_specs = (P("section", ("dp", "tp"), None, None), P("section", ("dp", "tp"), None, None))
    return jax.shard_map(shards, mesh=mesh, in_specs=in_specs, out_specs=out_specs, check_vma=False)
```

profile of v0, /device:TPU:0, one launch (start us, length us, event | category | flops | bytes accessed | tf_op | source)
XLA Modules:
  0.0 107.4 jit_solution(17784348810018977963)
XLA Ops:
  7.2 1.4 %fusion.18 = f32[128]{0:T(128)S(1)} fusion(bf16[1,1,128,2304]{3,2,1,0:T(8,128)(2,1)} %param.10), kind=kLoop, calls=%fused_computation.21 | loop fusion | flops 884608 | bytes 590336 | tf_op jit(solution)/shard_map/reduce_sum | solution.py:21
  8.7 0.7 reduce
  9.4 2.1 %fusion.20 = bf16[128,2304]{1,0:T(8,128)(2,1)} fusion(bf16[1,1,128,2304]{3,2,1,0:T(8,128)(2,1)} %param.10, f32[2304]{0:T(1024)S(1)} %reduce, f32[128]{0:T(128)S(1)} %add_rsqrt_fusion.1), kind=kLoop, calls=%fused_computation.23 | loop fusion | flops 1179648 | bytes 1189376 | tf_op jit(solution)/shard_map/convert_element_type | solution.py:45
  11.5 6.8 %copy.33 = bf16[1024,2304]{1,0:T(8,128)(2,1)} copy(bf16[1024,2304]{0,1:T(8,128)(2,1)} %bitcast.64) | data formatting | bytes 9437184 | tf_op jit(solution)/shard_map/dot_general | solution.py:49
  18.3 4.4 %copy.30 = bf16[512,2304]{1,0:T(8,128)(2,1)} copy(bf16[512,2304]{0,1:T(8,128)(2,1)} %bitcast.66) | data formatting | bytes 4718592 | tf_op jit(solution)/shard_map/dot_general | solution.py:52
  22.9 0.7 broadcast_and_fusion
  23.6 0.3 multiply_cosine_fusion
  23.9 13.2 %all-gather.2.cloned.1.call-done = bf16[256,2304]{1,0:T(8,128)(2,1)} async-done(((bf16[128,2304]{1,0:T(8,128)(2,1)}), bf16[256,2304]{1,0:T(8,128)(2,1)}) %all-gather.2.cloned.1.call-update) | async-done | bytes 1179664 | tf_op jit(solution)/shard_map/all_gather | solution.py:46
  37.1 4.1 %fusion.22 = f32[256,8,128]{0,2,1:T(8,128)S(1)} fusion(bf16[8,128,2304]{2,1,0:T(8,128)(2,1)} %bitcast.65, bf16[256,2304]{1,0:T(8,128)(2,1)} %all-gather.2.cloned.1.call-done), kind=kOutput, calls=%fused_computation.25 | convolution fusion | flops 1207959552 | bytes 6946816 | tf_op jit(solution)/shard_map/dot_general | solution.py:49
  41.6 2.8 %fusion.24 = f32[256,4,128]{0,2,1:T(8,128)S(1)} fusion(bf16[4,128,2304]{2,1,0:T(8,128)(2,1)} %bitcast.67, bf16[256,2304]{1,0:T(8,128)(2,1)} %all-gather.2.cloned.1.call-done), kind=kOutput, calls=%fused_computation.27 | convolution fusion | flops 603979776 | bytes 4063232 | tf_op jit(solution)/shard_map/dot_general | solution.py:52
  44.7 2.8 %fusion.13 = bf16[256,512]{1,0:T(8,128)(2,1)} fusion(bf16[256,2304]{1,0:T(8,128)(2,1)} %all-gather.2.cloned.1.call-done, bf16[1,2304,512]{2,1,0:T(8,128)(2,1)S(1)} %copy-done), kind=kOutput, calls=%fused_computation.18 | convolution fusion | flops 604110848 | bytes 3801088 | tf_op jit(solution)/shard_map/dot_general | solution.py:55
  47.4 1.0 reshape.149
  48.4 1.5 %fusion.11 = f32[2,4,2,128,128]{3,4,2,1,0:T(8,128)} fusion(bf16[2,128,4,2,128]{1,0,4,3,2:T(2,128)(2,1)S(1)} %reshape.151, pred[2,128,128]{1,2,0:T(8,128)(4,1)S(1)} %copy-done.2, bf16[2,128,4,128,1]{1,0,3,2,4:T(2,128)(2,1)S(1)} %bitcast.68), kind=kOutput, calls=%fused_computation.15 | convolution fusion | flops 67895296 | bytes 1867776 | tf_op jit(solution)/shard_map/bqkgd,bskd->bkgqs/dot_general | solution.py:75
  49.9 1.9 %fusion.12 = bf16[2,128,4,2,128]{1,4,3,2,0:T(8,128)(2,1)S(1)} fusion(f32[2,4,2,128,128]{3,4,2,1,0:T(8,128)} %fusion.11, bf16[2,128,4,128,1]{3,2,1,0,4:T(4,128)(2,1)S(1)} %bitcast.69), kind=kOutput, calls=%fused_computation.17 | convolution fusion | flops 67897472 | bytes 1835008 | tf_op jit(solution)/shard_map/bkgqs,bskd->bqkgd/dot_general | solution.py:86
  51.8 0.4 copy.24
  52.3 0.4 reshape.152
  52.6 4.7 %fusion.2 = bf16[256,2304]{1,0:T(8,128)(2,1)} fusion(bf16[256,1024]{1,0:T(8,128)(2,1)S(1)} %reshape.152, bf16[1,1024,2304]{2,1,0:T(8,128)(2,1)} %param.19), kind=kOutput, calls=%fused_computation.2 | convolution fusion | flops 1208549376 | bytes 6422528 | tf_op jit(solution)/shard_map/dot_general | solution.py:91
  57.4 0.7 copy-done.3
  58.1 21.3 %reduce-scatter.2.cloned.1.call-done = bf16[128,2304]{1,0:T(8,128)(2,1)} async-done(((bf16[256,2304]{1,0:T(8,128)(2,1)}), bf16[128,2304]{1,0:T(8,128)(2,1)}) %reduce-scatter.2.cloned.1.call-update) | async-done | bytes 589840 | tf_op jit(solution)/shard_map/reduce_scatter | solution.py:90
  79.4 1.3 %fusion.16 = f32[128]{0:T(128)S(1)} fusion(bf16[128,2304]{1,0:T(8,128)(2,1)} %reduce-scatter.2.cloned.1.call-done), kind=kLoop, calls=%fused_computation.19 | loop fusion | flops 884608 | bytes 590336 | tf_op jit(solution)/shard_map/reduce_sum | solution.py:21
  80.7 2.2 %fusion.42 = (bf16[1,128,2304]{2,1,0:T(8,128)(2,1)S(1)}, bf16[1,1,128,2304]{3,2,1,0:T(8,128)(2,1)}) fusion(f32[2304]{0:T(1024)S(1)} %reduce.1, f32[128]{0:T(128)S(1)} %add_rsqrt_fusion, bf16[128,2304]{1,0:T(8,128)(2,1)} %reduce-scatter.2.cloned.1.call-done, bf16[1,1,128,2304]{3,2,1,0:T(8,128)(2,1)S(1)} %copy-done.1), kind=kLoop, calls=%fused_computation.57 | loop fusion | flops 1769472 | bytes 2369024 | tf_op jit(solution)/shard_map/reshape | solution.py:96
  82.9 3.4 %collective-permute-start = (bf16[1,128,2304]{2,1,0:T(8,128)(2,1)S(1)}, bf16[1,128,2304]{2,1,0:T(8,128)(2,1)S(1)}, u32[]{:S(2)}, u32[]{:S(2)}) collective-permute-start(bf16[1,128,2304]{2,1,0:T(8,128)(2,1)S(1)} %get-tuple-element.2), channel_id=1, source_target_pairs={{0,8},{8,16},{16,24},{1,9},{9,17},{17,25},{2,10},{10,18},{18,26},{... | collective-permute-start | bytes 1769480 | tf_op jit(solution)/shard_map/ppermute | solution.py:17
  86.4 12.2 %collective-permute-done = bf16[1,128,2304]{2,1,0:T(8,128)(2,1)S(1)} collective-permute-done((bf16[1,128,2304]{2,1,0:T(8,128)(2,1)S(1)}, bf16[1,128,2304]{2,1,0:T(8,128)(2,1)S(1)}, u32[]{:S(2)}, u32[]{:S(2)}) %collective-permute-start) | collective-permute-done | bytes 589856 | tf_op jit(solution)/shard_map/ppermute | solution.py:17
  98.7 1.9 %fusion.26 = bf16[1,1,128,2304]{3,2,1,0:T(8,128)(2,1)} fusion(bf16[1,128,2304]{2,1,0:T(8,128)(2,1)S(1)} %collective-permute-done, bf16[6,1,128,2304]{3,2,1,0:T(8,128)(2,1)} %param.11, s32[]{:T(128)S(6)} %select_n.44, pred[]{:T(512)S(6)} %eq.5), kind=kLoop, calls=%fused_computation.31 | loop fusion | flops 294912 | bytes 1769477 | tf_op jit(solution)/shard_map/broadcast_in_dim | solution.py:125
  (28 shorter events, 0.8 us)
Async XLA Ops:
  7.2 37.5 %copy-start = (bf16[1,2304,512]{2,1,0:T(8,128)(2,1)S(1)}, bf16[1,2304,512]{2,1,0:T(8,128)(2,1)}, u32[]{:S(2)}) copy-start(bf16[1,2304,512]{2,1,0:T(8,128)(2,1)} %param.18) | copy-start | bytes 7077892
  7.2 30.0 %all-gather.2.cloned.1.call-start = ((), (), s32[]{:S(2)}) async-start(), calls=%async_computation.1 | async-start | bytes 1769472 | tf_op jit(solution)/shard_map/all_gather | solution.py:46
  11.5 67.9 %reduce-scatter.2.cloned.1.call-start = ((), (), s32[]{:S(2)}) async-start(), calls=%async_computation.2 | async-start | bytes 1769472 | tf_op jit(solution)/shard_map/reduce_scatter | solution.py:90
  18.3 4.4 %copy-start.5 = (s32[1,2]{1,0:T(1,128)S(1)}, s32[1,2]{1,0:T(1,128)}, u32[]{:S(2)}) copy-start(s32[1,2]{1,0:T(1,128)} %param.13) | copy-start | bytes 28
  44.6 3.8 %copy-start.2 = (pred[2,128,128]{1,2,0:T(8,128)(4,1)S(1)}, pred[2,128,128]{1,2,0:T(8,128)(4,1)}, u32[]{:S(2)}) copy-start(pred[2,128,128]{1,2,0:T(8,128)(4,1)} %broadcast_and_fusion) | copy-start | bytes 98308
  57.4 0.7 copy-start.3
  57.4 23.3 %copy-start.1 = (bf16[1,1,128,2304]{3,2,1,0:T(8,128)(2,1)S(1)}, bf16[1,1,128,2304]{3,2,1,0:T(8,128)(2,1)}, u32[]{:S(2)}) copy-start(bf16[1,1,128,2304]{3,2,1,0:T(8,128)(2,1)} %param.10) | copy-start | bytes 1769476
  80.7 5.6 %copy-start.4 = (s32[6]{0:T(128)S(1)}, s32[6]{0:T(128)}, u32[]{:S(2)}) copy-start(s32[6]{0:T(128)} %param.12) | copy-start | bytes 76
  82.9 15.8 %collective-permute-start = (bf16[1,128,2304]{2,1,0:T(8,128)(2,1)S(1)}, bf16[1,128,2304]{2,1,0:T(8,128)(2,1)S(1)}, u32[]{:S(2)}, u32[]{:S(2)}) collective-permute-start(bf16[1,128,2304]{2,1,0:T(8,128)(2,1)S(1)} %get-tuple-element.2), channel_id=1, source_target_pairs={{0,8},{8,16},{16,24},{1,9},{9,17},{17,25},{2,10},{10,18},{18,26},{... | collective-permute-start | bytes 1769480 | tf_op jit(solution)/shard_map/ppermute | solution.py:17
Sparse Core Ops, SparseCore 0:
  11.6 25.4 all-gather.1
  57.5 21.8 reduce-scatter.1
where the time goes:
time: 108 us; the launch traced here: 107 us
  waiting for transfers between devices  46.8 us (43%)
  matrix products  17.8 us (16%)
  between operations  14.3 us (13%)
  local copies, waits for them, and re-layouts  13.9 us (13%)
  other arithmetic  11.1 us (10%)
  starting transfers between devices  3.5 us (3%)
    reduce_scatter x1, waiting for transfers between devices, layer(): lax.psum_scatter(jnp.dot(mixed_flat, w_out, preferred_element_type=jnp.fl...  21.3 us
    all_gather x1, waiting for transfers between devices, layer(): normalized_input = lax.all_gather(normed_own, 'tp', axis=0, tiled=True)  13.2 us
    ppermute x1, waiting for transfers between devices, shifted(): return lax.ppermute(block, axis, route)  12.2 us
    dot_general x1, local copies, waits for them, and re-layouts, layer(): jnp.dot(normalized_input, w_query, preferred_element_type=jnp.float32)  6.8 us
    dot_general x1, matrix products, layer(): jnp.dot(mixed_flat, w_out, preferred_element_type=jnp.float32)  4.73 us
    dot_general x1, local copies, waits for them, and re-layouts, layer(): jnp.dot(normalized_input, key_weight, preferred_element_type=jnp.float32)  4.4 us
    dot_general x1, matrix products, layer(): jnp.dot(normalized_input, w_query, preferred_element_type=jnp.float32)  4.12 us
    ppermute x1, starting transfers between devices, shifted(): return lax.ppermute(block, axis, route)  3.42 us
  transfers between devices with their start and end apart: 3, of which 3 were waited for; matrix products, arithmetic and copies ran while one was open for 12% of the time, Pallas kernels for 0%

commit v1 on v0

v1 whole, which is shorter than its diff:
```python
import functools

import jax
import jax.numpy as jnp
import numpy as np
from jax import lax
from jax.experimental import pallas as pl
from jax.experimental.pallas import tpu as pltpu
from jax.sharding import PartitionSpec as P

HEAD_WIDTH = 128
EPSILON = 1e-06
SOFT_CAP = 50.0
QUERY_SCALE = 144.0 ** (-0.5)

VMEM = pl.BlockSpec(memory_space=pltpu.VMEM)
SMEM = pl.BlockSpec(memory_space=pltpu.SMEM)
HBM = pl.BlockSpec(memory_space=pl.ANY)
F32 = jnp.float32
BF16 = jnp.bfloat16


def vmem_out(shape, dtype=BF16):
    return pltpu.VMEM(shape, dtype)


def pieces_of(seq_len):
    half, quarter = seq_len // 2, seq_len // 4
    return (
        (0, half, ((0, half),)),
        (half, seq_len, ((half, half + quarter), (half + quarter, seq_len))),
    )


def rotary_tables(seq_len):
    half = HEAD_WIDTH // 2
    freq = np.float32(10000.0) ** (np.float32(-2.0) * np.arange(half, dtype=np.float32) / np.float32(HEAD_WIDTH))
    angle = np.arange(seq_len, dtype=np.float32)[:, None] * freq[None, :]
    cosine, sine = np.cos(angle), np.sin(angle)
    return (
        np.concatenate([cosine, cosine], 1).astype(np.float32),
        np.concatenate([-sine, sine], 1).astype(np.float32),
    )


def rotate(values, cosine, sine):
    return values * cosine + pltpu.roll(values, HEAD_WIDTH // 2, 1) * sine


def attend(normed, first, length, cosine, sine, prev, wq, wk, wv, wo, ready, sinks, kv_sinks):
    rows = normed.shape[0]
    kv_cols = wk.shape[1]
    heads_kv = kv_cols // HEAD_WIDTH
    group = wq.shape[1] // kv_cols
    total = first + rows
    dot = functools.partial(jnp.dot, preferred_element_type=F32)
    ready("k")
    keys = dot(normed, wk[...])
    ready("v")
    vals = dot(normed, wv[...]).astype(BF16)
    keys = [
        rotate(keys[:, g * HEAD_WIDTH : (g + 1) * HEAD_WIDTH], cosine, sine).astype(BF16)
        for g in range(heads_kv)
    ]
    if kv_sinks is not None:
        for g in range(heads_kv):
            kv_sinks[0][:, g * HEAD_WIDTH : (g + 1) * HEAD_WIDTH] = keys[g]
        kv_sinks[1][...] = vals
    q_pos = lax.broadcasted_iota(jnp.int32, (rows, total), 0) + first
    k_pos = lax.broadcasted_iota(jnp.int32, (rows, total), 1)
    allowed = (k_pos <= q_pos) & (k_pos < length)
    allowed = jnp.concatenate([allowed] * group, 0)
    mixed = []
    for g in range(heads_kv):
        ready("q", g)
        width = group * HEAD_WIDTH
        q = dot(normed, wq[:, g * width : (g + 1) * width])
        q = jnp.concatenate(
            [rotate(q[:, j * HEAD_WIDTH : (j + 1) * HEAD_WIDTH], cosine, sine) for j in range(group)], 0
        ).astype(BF16)
        kg, vg = keys[g], vals[:, g * HEAD_WIDTH : (g + 1) * HEAD_WIDTH]
        if prev is not None:
            cols = slice(g * HEAD_WIDTH, (g + 1) * HEAD_WIDTH)
            kg = jnp.concatenate([prev[0][:, cols], kg], 0)
            vg = jnp.concatenate([prev[1][:, cols], vg], 0)
        scores = lax.dot_general(q, kg, (((1,), (1,)), ((), ())), preferred_element_type=F32)
        capped = SOFT_CAP * jnp.tanh(scores * (QUERY_SCALE / SOFT_CAP))
        raised = jnp.where(allowed, jnp.exp(capped), 0.0)
        probs = (raised / jnp.sum(raised, -1, keepdims=True)).astype(BF16)
        out = dot(probs, vg).astype(BF16)
        mixed += [out[j * rows : (j + 1) * rows] for j in range(group)]
    mixed = jnp.concatenate(mixed, 1)
    width = wo.shape[1]
    step = next(s for s in (768, 512, 384, 256, 128, width) if width % s == 0)
    for n, c in enumerate(range(0, width, step)):
        ready("o", n)
        part = dot(mixed, wo[:, c : c + step]).astype(BF16)
        for (a, b), sink in sinks:
            sink[:, c : c + step] = part[a - first : b - first]


def normalize(values, gain):
    return values * lax.rsqrt(jnp.mean(values * values, -1, keepdims=True) + EPSILON) * gain


def own_kernel(axis, spans, nx, n_out, *refs):
    xs, refs = refs[:nx], refs[nx:]
    gain, cosine, sine, lengths, hq, hk, hv, ho = refs[:8]
    outs = refs[8 : 8 + n_out]
    wq, wk, wv, wo = refs[8 + n_out : 12 + n_out]
    sems = refs[12 + n_out]
    kv_cols = wk.shape[1]
    width = wq.shape[1] // (kv_cols // HEAD_WIDTH)
    model = wo.shape[1]
    step = next(s for s in (768, 512, 384, 256, 128, model) if model % s == 0)
    copies = {("k",): (hk, wk, 0, kv_cols), ("v",): (hv, wv, 0, kv_cols)}
    for g in range(kv_cols // HEAD_WIDTH):
        copies["q", g] = (hq, wq, g * width, width)
    for n in range(model // step):
        copies["o", n] = (ho, wo, n * step, step)
    started = {}
    for i, (name, (src, dst, c, w)) in enumerate(copies.items()):
        started[name] = pltpu.make_async_copy(src.at[:, c : c + w], dst.at[:, c : c + w], sems.at[i])
        started[name].start()
    me = lax.axis_index(axis)
    normed = jnp.concatenate([normalize(x[...].astype(F32), gain[...]).astype(BF16) for x in xs], 0)
    attend(
        normed, 0, lengths[0, me], cosine[...], sine[...], None, wq, wk, wv, wo,
        lambda *name: started[name].wait(), list(zip(spans, outs)), None,
    )


def peer_kernel(axis, distance, first, spans, keep, *refs):
    x, gain, cosine, sine, lengths, wq, wk, wv, wo = refs[:9]
    refs = refs[9:]
    prev = None
    if first:
        prev, refs = (refs[0], refs[1]), refs[2:]
    outs, refs = refs[: len(spans)], refs[len(spans) :]
    n = lengths.shape[1]
    owner = lax.rem(lax.axis_index(axis) + (n - distance), n)
    normed = normalize(x[...].astype(F32), gain[...]).astype(BF16)
    rows = x.shape[0]
    attend(
        normed, first, lengths[0, owner], cosine[first : first + rows, :], sine[first : first + rows, :],
        prev, wq, wk, wv, wo, lambda *name: None, list(zip(spans, outs)), refs[:2] if keep else None,
    )


def finish_kernel(offset, *refs):
    own, x, gain = refs[:3]
    others, out = refs[3:-1], refs[-1]
    rows = own.shape[0]
    branch = own[...].astype(F32)
    for other in others:
        branch = branch + other[...].astype(F32)
    held = x[offset : offset + rows, :].astype(F32)
    out[...] = (held + normalize(branch, gain[...])).astype(BF16)


def store_kernel(spans, *refs):
    pieces, out, sems = refs[: len(spans)], refs[-2], refs[-1]
    copies = [
        pltpu.make_async_copy(p, out.at[0, 0, a:b], sems.at[i])
        for i, (p, (a, b)) in enumerate(zip(pieces, spans))
    ]
    for c in copies:
        c.start()
    for c in copies:
        c.wait()


def advance_kernel(axis, spans, *refs):
    pieces, fresh, out, sems = refs[: len(spans)], refs[-3], refs[-2], refs[-1]
    first = lax.axis_index(axis) == 0

    @pl.when(first)
    def _():
        copy = pltpu.make_async_copy(fresh, out.at[0, 0], sems.at[0])
        copy.start()
        copy.wait()

    @pl.when(jnp.logical_not(first))
    def _():
        store_kernel(spans, *pieces, out, sems)


def fresh_kernel(order, fresh_rows, out, sem):
    copy = pltpu.make_async_copy(fresh_rows.at[order[0], 0], out, sem)
    copy.start()
    copy.wait()


def split_kernel(spans, x, *refs):
    outs, sems = refs[:-1], refs[-1]
    copies = [
        pltpu.make_async_copy(x.at[0, 0, a:b], out, sems.at[i])
        for i, (out, (a, b)) in enumerate(zip(outs, spans))
    ]
    for c in copies:
        c.start()
    for c in copies:
        c.wait()


def call(kernel, name, out_shape, in_specs, out_specs, args, scratch=(), us=1.0, limit=16 << 20):
    return pl.pallas_call(
        kernel,
        out_shape=out_shape,
        in_specs=in_specs,
        out_specs=out_specs,
        scratch_shapes=list(scratch),
        name=name,
        cost_estimate=pl.CostEstimate(flops=int(us * 1e7), bytes_accessed=1024, transcendentals=0),
        compiler_params=pltpu.CompilerParams(vmem_limit_bytes=limit),
    )(*args)


def shards(
    incoming,
    fresh_rows,
    entry_order,
    flight_lengths,
    pre_gain,
    post_gain,
    w_query,
    key_weight,
    value_weight,
    w_out,
):
    seq_len, model = incoming.shape[2:]
    chunks = pieces_of(seq_len)
    spans = [span for _, _, inner in chunks for span in inner]
    n_tp = lax.axis_size("tp")
    n_section = lax.axis_size("section")
    wq, wk, wv, wo = w_query[0], key_weight[0], value_weight[0], w_out[0]
    kv_cols = wk.shape[1]
    cosine, sine = (jnp.asarray(t) for t in rotary_tables(seq_len))
    dma = pltpu.SemaphoreType.DMA

    xs = call(
        functools.partial(split_kernel, [(a, b) for a, b, _ in chunks]), "split",
        [vmem_out((b - a, model)) for a, b, _ in chunks], [HBM], [VMEM] * len(chunks),
        [incoming], [dma((len(chunks),))],
    )
    out_of = {d: [(i, (i + d) % n_tp) for i in range(n_tp)] for d in range(n_tp)}
    arrived = {d: [lax.ppermute(x, "tp", out_of[d]) for x in xs] for d in range(1, n_tp)}

    n_copies = 2 + kv_cols // HEAD_WIDTH + model // 128
    own = call(
        functools.partial(own_kernel, "tp", spans, len(xs), len(spans)), "own",
        [vmem_out((b - a, model)) for a, b in spans] + [vmem_out(w.shape) for w in (wq, wk, wv, wo)],
        [VMEM] * len(xs) + [VMEM, VMEM, VMEM, SMEM] + [HBM] * 4, [VMEM] * (len(spans) + 4),
        [*xs, pre_gain, cosine, sine, flight_lengths, wq, wk, wv, wo], [dma((n_copies,))], us=6.0,
    )
    own, weights = own[: len(spans)], own[len(spans) :]
    fresh = call(
        fresh_kernel, "fresh", vmem_out((seq_len, model)), [SMEM, HBM], VMEM,
        [entry_order, fresh_rows], [dma],
    )

    back = {span: [] for span in spans}
    for d in range(1, n_tp):
        kept = []
        for c, (first, last, inner) in enumerate(chunks):
            keep = c + 1 < len(chunks)
            shapes = [vmem_out((b - a, model)) for a, b in inner]
            shapes += [vmem_out((last - first, kv_cols))] * 2 if keep else []
            prev = []
            if first:
                prev = [jnp.concatenate([k[i] for k in kept], 0) if len(kept) > 1 else kept[0][i] for i in range(2)]
            done = call(
                functools.partial(peer_kernel, "tp", d, first, inner, keep), f"peer{c}",
                shapes, [VMEM] * 4 + [SMEM] + [VMEM] * (4 + len(prev)), [VMEM] * len(shapes),
                [arrived[d][c], pre_gain, cosine, sine, flight_lengths, *weights, *prev], us=5.0,
            )
            kept.append(done[len(inner) :])
            for span, part in zip(inner, done):
                back[span].append(lax.ppermute(part, "tp", [(t, s) for s, t in out_of[d]]))

    produced, moved = [], []
    line = [(i, i + 1) for i in range(n_section - 1)]
    for c, (first, last, inner) in enumerate(chunks):
        for span in inner:
            i = spans.index(span)
            piece = call(
                functools.partial(finish_kernel, span[0] - first), "finish",
                vmem_out((span[1] - span[0], model)), [VMEM] * (3 + len(back[span])), VMEM,
                [own[i], xs[c], post_gain, *back[span]], us=1.0,
            )
            produced.append(piece)
            moved.append(lax.ppermute(piece, "section", line))
    full = jax.ShapeDtypeStruct(incoming.shape, incoming.dtype)
    stored = call(
        functools.partial(store_kernel, spans), "store", full, [VMEM] * len(spans), HBM,
        produced, [dma((len(spans),))],
    )
    advanced = call(
        functools.partial(advance_kernel, "section", spans), "advance", full,
        [VMEM] * (len(spans) + 1), HBM, [*moved, fresh], [dma((len(spans),))],
    )
    return stored, advanced


def solution(mesh):
    in_specs = (
        P("section", ("dp", "tp"), None, None),
        P(None, ("dp", "tp"), None, None),
        P("dp"),
        P("section", "dp"),
        P("section", None),
        P("section", None),
        P("section", None, "tp"),
        P("section", None, "tp"),
        P("section", None, "tp"),
        P("section", "tp", None),
    )
    out_specs = (P("section", ("dp", "tp"), None, None), P("section", ("dp", "tp"), None, None))
    return jax.shard_map(shards, mesh=mesh, in_specs=in_specs, out_specs=out_specs, check_vma=False)
```

time: 108 us -> 55.1 us (0.51)
  waiting for transfers between devices: 46.8 us -> 2.28 us
  Pallas kernels: 0 us -> 21.7 us
  matrix products: 17.8 us -> 0 us
  starting transfers between devices: 3.5 us -> 17.7 us
  between operations: 14.3 us -> 0.79 us
  other arithmetic: 11.1 us -> 0 us
  local copies, waits for them, and re-layouts: 13.9 us -> 12.1 us
    pallas_call x0 -> x10, Pallas kernels: none -> 21.7 us  [call(): pl.pallas_call(kernel, out_shape=out_shape, in_specs=in_specs, out_specs=...]
    reduce_scatter x1 -> x0, waiting for transfers between devices: 21.3 us -> none  [layer(): lax.psum_scatter(jnp.dot(mixed_flat, w_out, preferred_element_type=jnp.fl...]
    dot_general x6 -> x0, matrix products: 17.8 us -> none  [the longest x1 4.73 us: layer(): jnp.dot(mixed_flat, w_out, preferred_element_type=jnp.float32)]
    ppermute x1 -> x8, starting transfers between devices: 3.42 us -> 17.7 us  [the longest x3 10.5 us: shards(): moved.append(lax.ppermute(piece, 'section', line))]
    all_gather x1 -> x0, waiting for transfers between devices: 13.2 us -> none  [layer(): normalized_input = lax.all_gather(normed_own, 'tp', axis=0, tiled=True)]
    unnamed x12 -> x24, local copies, waits for them, and re-layouts: 0.7 us -> 12.1 us
    dot_general x2 -> x0, local copies, waits for them, and re-layouts: 11.2 us -> none  [the longest x1 6.8 us: layer(): jnp.dot(normalized_input, w_query, preferred_element_type=jnp.float32)]
    ppermute x1 -> x8, waiting for transfers between devices: 12.2 us -> 2.28 us  [the longest x3 1.74 us: shards(): moved.append(lax.ppermute(piece, 'section', line))]
  transfers between devices with their start and end apart: 3 -> 8, of which waited for: 3 -> 3; matrix products, arithmetic and copies ran while one was open for 12% -> 0% of each run, Pallas kernels for 0% -> 38%
where the time goes in v1:
time: 55.1 us; the launch traced here: 54.6 us
  Pallas kernels  21.7 us (39%)
  starting transfers between devices  17.7 us (32%)
  local copies, waits for them, and re-layouts  12.1 us (22%)
  waiting for transfers between devices  2.28 us (4%)
  between operations  0.79 us (1%)
    pallas_call x10, Pallas kernels, call(): pl.pallas_call(kernel, out_shape=out_shape, in_specs=in_specs, out_specs=...  21.7 us
    unnamed x24, local copies, waits for them, and re-layouts  12.1 us
    ppermute x3, starting transfers between devices, shards(): moved.append(lax.ppermute(piece, 'section', line))  10.5 us
    ppermute x3, starting transfers between devices, shards(): back[span].append(lax.ppermute(part, 'tp', [(t, s) for s, t in out_of[d]]))  4.1 us
    ppermute x2, starting transfers between devices, shards(): lax.ppermute(x, 'tp', out_of[d])  3.14 us
    ppermute x3, waiting for transfers between devices, shards(): moved.append(lax.ppermute(piece, 'section', line))  1.74 us
  transfers between devices with their start and end apart: 8, of which 3 were waited for; matrix products, arithmetic and copies ran while one was open for 0% of the time, Pallas kernels for 38%

profile of v1, /device:TPU:0, one launch (start us, length us, event | category | flops | bytes accessed | tf_op | source)
XLA Modules:
  0.0 54.6 jit_solution(9673708416312084524)
XLA Ops:
  0.6 1.1 %copy-done.7 = bf16[1,1,128,2304]{3,2,1,0:T(8,128)(2,1)S(1)} copy-done((bf16[1,1,128,2304]{3,2,1,0:T(8,128)(2,1)S(1)}, bf16[1,1,128,2304]{3,2,1,0:T(8,128)(2,1)}, u32[]{:S(2)}) %copy-start.7) | copy-done | bytes 589848
  1.8 3.1 %collective-permute-start = (bf16[64,2304]{1,0:T(8,128)(2,1)S(1)}, bf16[64,2304]{1,0:T(8,128)(2,1)S(1)}, u32[]{:S(2)}, u32[]{:S(2)}) collective-permute-start(bf16[64,2304]{1,0:T(8,128)(2,1)S(1)} %get-tuple-element.16.refs_0_.refs_1_), channel_id=1, source_target_pairs={{0,4},{4,0},{1,5},{5,1},{2,6},{6,2},{3,7},{7,3},{8,12},{12,8},{9,1... | collective-permute-start | bytes 884744 | tf_op jit(solution)/shard_map/ppermute | solution.py:247
  5.0 2.3 %copy-done = bf16[1,2304,1024]{2,1,0:T(8,128)(2,1)S(1)} copy-done((bf16[1,2304,1024]{2,1,0:T(8,128)(2,1)S(1)}, bf16[1,2304,1024]{2,1,0:T(8,128)(2,1)}, u32[]{:S(2)}) %copy-start) | copy-done | bytes 4718616
  7.3 2.3 %copy-done.1 = bf16[1,1024,2304]{2,1,0:T(8,128)(2,1)S(1)} copy-done((bf16[1,1024,2304]{2,1,0:T(8,128)(2,1)S(1)}, bf16[1,1024,2304]{2,1,0:T(8,128)(2,1)}, u32[]{:S(2)}) %copy-start.1) | copy-done | bytes 4718616
  9.7 1.7 %copy-done.3 = bf16[1,2304,512]{2,1,0:T(8,128)(2,1)S(1)} copy-done((bf16[1,2304,512]{2,1,0:T(8,128)(2,1)S(1)}, bf16[1,2304,512]{2,1,0:T(8,128)(2,1)}, u32[]{:S(2)}) %copy-start.3) | copy-done | bytes 2359320
  11.3 1.7 %copy-done.4 = bf16[1,2304,512]{2,1,0:T(8,128)(2,1)S(1)} copy-done((bf16[1,2304,512]{2,1,0:T(8,128)(2,1)S(1)}, bf16[1,2304,512]{2,1,0:T(8,128)(2,1)}, u32[]{:S(2)}) %copy-start.4) | copy-done | bytes 2359320
  13.0 0.8 %copy-done.5 = f32[128,128]{1,0:T(8,128)S(1)} copy-done((f32[128,128]{1,0:T(8,128)S(1)}, f32[128,128]{1,0:T(8,128)}, u32[]{:S(2)}) %copy-start.5) | copy-done | bytes 65560
  13.8 0.8 %copy-done.6 = f32[128,128]{1,0:T(8,128)S(1)} copy-done((f32[128,128]{1,0:T(8,128)S(1)}, f32[128,128]{1,0:T(8,128)}, u32[]{:S(2)}) %copy-start.6) | copy-done | bytes 65560
  14.7 0.7 %copy-done.8 = f32[1,2304]{1,0:T(1,128)S(1)} copy-done((f32[1,2304]{1,0:T(1,128)S(1)}, f32[1,2304]{1,0:T(1,128)}, u32[]{:S(2)}) %copy-start.8) | copy-done | bytes 9240
  15.4 0.7 %copy-done.10 = s32[1,2]{1,0:T(1,128)S(1)} copy-done((s32[1,2]{1,0:T(1,128)S(1)}, s32[1,2]{1,0:T(1,128)}, u32[]{:S(2)}) %copy-start.10) | copy-done | bytes 32
  16.0 8.1 %own.1 = (bf16[64,2304]{1,0:T(8,128)(2,1)S(1)}, bf16[32,2304]{1,0:T(8,128)(2,1)S(1)}, bf16[32,2304]{1,0:T(8,128)(2,1)S(1)}, bf16[2304,1024]{1,0:T(8,128)(2,1)S(1...) custom-call(bf16[64,2304]{1,0:T(8,128)(2,1)S(1)} %get-tuple-element.16.refs_0_.refs_, ...), custom_call_target="tpu_custom_call" | custom-call | flops 60000000 | bytes 1024 | tf_op jit(solution)/shard_map/own/pallas_call | solution.py:207
  24.1 5.3 %peer0.1 = (bf16[64,2304]{1,0:T(8,128)(2,1)S(1)}, bf16[64,512]{1,0:T(8,128)(2,1)S(1)}, bf16[64,512]{1,0:T(8,128)(2,1)S(1)}) custom-call(bf16[64,2304]{1,0:T(8,128)(2,1)S(1)} %collective-permute-done.refs_0_, f32[1,2304]{1,0:T(1,128)S(1)} %copy-done.8, f32[128,128]{1,0:T(8,128)S(1)} %copy-done.5, f32[128,128]{1,0:T(8,128)S(1)} %copy-done.6, ...), custom_call_target="tpu_custom_call" | custom-call | flops 50000000 | bytes 1024 | tf_op jit(solution)/shard_map/peer0/pallas_call | solution.py:207
  29.4 2.0 %collective-permute-start.1 = (bf16[64,2304]{1,0:T(8,128)(2,1)S(1)}, bf16[64,2304]{1,0:T(8,128)(2,1)S(1)}, u32[]{:S(2)}, u32[]{:S(2)}) collective-permute-start(bf16[64,2304]{1,0:T(8,128)(2,1)S(1)} %get-tuple-element.23), channel_id=1, source_target_pairs={{4,0},{0,4},{5,1},{1,5},{6,2},{2,6},{7,3},{3,7},{12,8},{8,12},{13,... | collective-permute-start | bytes 884744 | tf_op jit(solution)/shard_map/ppermute | solution.py:279
  31.4 5.3 %peer1.1 = (bf16[32,2304]{1,0:T(8,128)(2,1)S(1)}, bf16[32,2304]{1,0:T(8,128)(2,1)S(1)}) custom-call(bf16[64,2304]{1,0:T(8,128)(2,1)S(1)} %collective-permute-done.2.refs_0_, f32[1,2304]{1,0:T(1,128)S(1)} %copy-done.8, f32[128,128]{1,0:T(8,128)S(1)} %copy-done.5, f32[128,128]{1,0:T(8,128)S(1)} %copy-done.6, s32[1,2]{1,0:T(1,128)S(1)} %copy-done.10, ...), custom_call_target="tpu_custom_call" | custom-call | flops 50000000 | bytes 1024 | tf_op jit(solution)/shard_map/peer1/pallas_call | solution.py:207
  36.8 1.9 %collective-permute-start.4 = (bf16[32,2304]{1,0:T(8,128)(2,1)S(1)}, bf16[32,2304]{1,0:T(8,128)(2,1)S(1)}, u32[]{:S(2)}, u32[]{:S(2)}) collective-permute-start(bf16[32,2304]{1,0:T(8,128)(2,1)S(1)} %get-tuple-element.29), channel_id=1, source_target_pairs={{4,0},{0,4},{5,1},{1,5},{6,2},{2,6},{7,3},{3,7},{12,8},{8,12},{13,... | collective-permute-start | bytes 442376 | tf_op jit(solution)/shard_map/ppermute | solution.py:279
  38.8 0.2 finish.3.refs_0_
  39.1 3.5 %collective-permute-start.5 = (bf16[64,2304]{1,0:T(8,128)(2,1)S(1)}, bf16[64,2304]{1,0:T(8,128)(2,1)S(1)}, u32[]{:S(2)}, u32[]{:S(2)}) collective-permute-start(bf16[64,2304]{1,0:T(8,128)(2,1)S(1)} %finish.3.refs_0_), channel_id=1, source_target_pairs={{0,8},{8,16},{16,24},{1,9},{9,17},{17,25},{2,10},{10,18},{18,26},{... | collective-permute-start | bytes 884744 | tf_op jit(solution)/shard_map/ppermute | solution.py:292
  42.6 0.5 collective-permute-done.3.refs_3_
  43.3 3.5 %collective-permute-start.6 = (bf16[32,2304]{1,0:T(8,128)(2,1)S(1)}, bf16[32,2304]{1,0:T(8,128)(2,1)S(1)}, u32[]{:S(2)}, u32[]{:S(2)}) collective-permute-start(bf16[32,2304]{1,0:T(8,128)(2,1)S(1)} %finish.4.refs_1_), channel_id=1, source_target_pairs={{0,8},{8,16},{16,24},{1,9},{9,17},{17,25},{2,10},{10,18},{18,26},{... | collective-permute-start | bytes 442376 | tf_op jit(solution)/shard_map/ppermute | solution.py:292
  46.9 3.5 %collective-permute-start.7 = (bf16[32,2304]{1,0:T(8,128)(2,1)S(1)}, bf16[32,2304]{1,0:T(8,128)(2,1)S(1)}, u32[]{:S(2)}, u32[]{:S(2)}) collective-permute-start(bf16[32,2304]{1,0:T(8,128)(2,1)S(1)} %finish.5.refs_2_), channel_id=1, source_target_pairs={{0,8},{8,16},{16,24},{1,9},{9,17},{17,25},{2,10},{10,18},{18,26},{... | collective-permute-start | bytes 442376 | tf_op jit(solution)/shard_map/ppermute | solution.py:292
  50.4 0.7 %fresh.1.refs_3_ = bf16[128,2304]{1,0:T(8,128)(2,1)S(1)} custom-call(s32[6]{0:T(128)S(1)} %copy-done.11, bf16[6,1,128,2304]{3,2,1,0:T(8,128)(2,1)S(1)} %copy-done.2), custom_call_target="tpu_custom_call" | custom-call | flops 10000000 | bytes 1024 | tf_op jit(solution)/shard_map/fresh/pallas_call | solution.py:207
  51.1 0.8 %store.1 = bf16[1,1,128,2304]{3,2,1,0:T(8,128)(2,1)} custom-call(bf16[64,2304]{1,0:T(8,128)(2,1)S(1)} %finish.3.refs_0_, bf16[32,2304]{1,0:T(8,128)(2,1)S(1)} %finish.4.refs_1_, bf16[32,2304]{1,0:T(8,128)(2,1)S(1)} %finish.5.refs_2_), custom_call_target="tpu_custom_call" | custom-call | flops 10000000 | bytes 1024 | tf_op jit(solution)/shard_map/store/pallas_call | solution.py:207
  52.1 1.6 %collective-permute-done.7.refs_2_ = bf16[32,2304]{1,0:T(8,128)(2,1)S(1)} collective-permute-done((bf16[32,2304]{1,0:T(8,128)(2,1)S(1)}, bf16[32,2304]{1,0:T(8,128)(2,1)S(1)}, u32[]{:S(2)}, u32[]{:S(2)}) %collective-permute-start.7) | collective-permute-done | bytes 147488 | tf_op jit(solution)/shard_map/ppermute | solution.py:292
  53.7 0.8 %advance.1 = bf16[1,1,128,2304]{3,2,1,0:T(8,128)(2,1)} custom-call(bf16[64,2304]{1,0:T(8,128)(2,1)S(1)} %collective-permute-done.5.refs_0_, bf16[32,2304]{1,0:T(8,128)(2,1)S(1)} %collective-permute-done.6.refs_1_, bf16[32,2304]{1,0:T(8,128)(2,1)S(1)} %collective-permute-done.7.refs_2_, bf16[128,2304]{1,0:T(8,128)(2,1)S(1)} %fresh.1.refs_3_), custom_call_target="tpu_custom_call" | custom-call | flops 10000000 | bytes 1024 | tf_op jit(solution)/shard_map/advance/pallas_call | solution.py:207
  (26 shorter events, 0.9 us)
Async XLA Ops:
  0.6 1.1 %copy-start.7 = (bf16[1,1,128,2304]{3,2,1,0:T(8,128)(2,1)S(1)}, bf16[1,1,128,2304]{3,2,1,0:T(8,128)(2,1)}, u32[]{:S(2)}) copy-start(bf16[1,1,128,2304]{3,2,1,0:T(8,128)(2,1)} %x.1) | copy-start | bytes 1769476
  1.8 22.3 %collective-permute-start = (bf16[64,2304]{1,0:T(8,128)(2,1)S(1)}, bf16[64,2304]{1,0:T(8,128)(2,1)S(1)}, u32[]{:S(2)}, u32[]{:S(2)}) collective-permute-start(bf16[64,2304]{1,0:T(8,128)(2,1)S(1)} %get-tuple-element.16.refs_0_.refs_1_), channel_id=1, source_target_pairs={{0,4},{4,0},{1,5},{5,1},{2,6},{6,2},{3,7},{7,3},{8,12},{12,8},{9,1... | collective-permute-start | bytes 884744 | tf_op jit(solution)/shard_map/ppermute | solution.py:247
  4.9 26.5 %collective-permute-start.2 = (bf16[64,2304]{1,0:T(8,128)(2,1)S(1)}, bf16[64,2304]{1,0:T(8,128)(2,1)S(1)}, u32[]{:S(2)}, u32[]{:S(2)}) collective-permute-start(bf16[64,2304]{1,0:T(8,128)(2,1)S(1)} %get-tuple-element.17.refs_1_), channel_id=1, source_target_pairs={{0,4},{4,0},{1,5},{5,1},{2,6},{6,2},{3,7},{7,3},{8,12},{12,8},{9,1... | collective-permute-start | bytes 884744 | tf_op jit(solution)/shard_map/ppermute | solution.py:247
  5.0 2.3 %copy-start = (bf16[1,2304,1024]{2,1,0:T(8,128)(2,1)S(1)}, bf16[1,2304,1024]{2,1,0:T(8,128)(2,1)}, u32[]{:S(2)}) copy-start(bf16[1,2304,1024]{2,1,0:T(8,128)(2,1)} %param.18) | copy-start | bytes 14155780
  7.3 2.3 %copy-start.1 = (bf16[1,1024,2304]{2,1,0:T(8,128)(2,1)S(1)}, bf16[1,1024,2304]{2,1,0:T(8,128)(2,1)}, u32[]{:S(2)}) copy-start(bf16[1,1024,2304]{2,1,0:T(8,128)(2,1)} %param.21) | copy-start | bytes 14155780
  9.7 1.7 %copy-start.3 = (bf16[1,2304,512]{2,1,0:T(8,128)(2,1)S(1)}, bf16[1,2304,512]{2,1,0:T(8,128)(2,1)}, u32[]{:S(2)}) copy-start(bf16[1,2304,512]{2,1,0:T(8,128)(2,1)} %param.19) | copy-start | bytes 7077892
  11.3 1.7 %copy-start.4 = (bf16[1,2304,512]{2,1,0:T(8,128)(2,1)S(1)}, bf16[1,2304,512]{2,1,0:T(8,128)(2,1)}, u32[]{:S(2)}) copy-start(bf16[1,2304,512]{2,1,0:T(8,128)(2,1)} %param.20) | copy-start | bytes 7077892
  13.0 0.8 %copy-start.5 = (f32[128,128]{1,0:T(8,128)S(1)}, f32[128,128]{1,0:T(8,128)}, u32[]{:S(2)}) copy-start(f32[128,128]{1,0:T(8,128)} %constant.4.clone.refs_3_.refs_2_) | copy-start | bytes 196612
  13.8 0.8 %copy-start.6 = (f32[128,128]{1,0:T(8,128)S(1)}, f32[128,128]{1,0:T(8,128)}, u32[]{:S(2)}) copy-start(f32[128,128]{1,0:T(8,128)} %constant.5.clone.refs_4_.refs_3_) | copy-start | bytes 196612
  14.7 0.7 %copy-start.8 = (f32[1,2304]{1,0:T(1,128)S(1)}, f32[1,2304]{1,0:T(1,128)}, u32[]{:S(2)}) copy-start(f32[1,2304]{1,0:T(1,128)} %refs_1_.3) | copy-start | bytes 27652
  15.4 0.7 %copy-start.10 = (s32[1,2]{1,0:T(1,128)S(1)}, s32[1,2]{1,0:T(1,128)}, u32[]{:S(2)}) copy-start(s32[1,2]{1,0:T(1,128)} %refs_4_.4) | copy-start | bytes 28
  29.4 9.4 %collective-permute-start.1 = (bf16[64,2304]{1,0:T(8,128)(2,1)S(1)}, bf16[64,2304]{1,0:T(8,128)(2,1)S(1)}, u32[]{:S(2)}, u32[]{:S(2)}) collective-permute-start(bf16[64,2304]{1,0:T(8,128)(2,1)S(1)} %get-tuple-element.23), channel_id=1, source_target_pairs={{4,0},{0,4},{5,1},{1,5},{6,2},{2,6},{7,3},{3,7},{12,8},{8,12},{13,... | collective-permute-start | bytes 884744 | tf_op jit(solution)/shard_map/ppermute | solution.py:279
  31.4 7.4 %copy-start.9 = (f32[1,2304]{1,0:T(1,128)S(1)}, f32[1,2304]{1,0:T(1,128)}, u32[]{:S(2)}) copy-start(f32[1,2304]{1,0:T(1,128)} %refs_2_.9) | copy-start | bytes 27652
  31.4 19.0 %copy-start.2 = (bf16[6,1,128,2304]{3,2,1,0:T(8,128)(2,1)S(1)}, bf16[6,1,128,2304]{3,2,1,0:T(8,128)(2,1)}, u32[]{:S(2)}) copy-start(bf16[6,1,128,2304]{3,2,1,0:T(8,128)(2,1)} %fresh_rows.1) | copy-start | bytes 10616836
  31.4 19.0 %copy-start.11 = (s32[6]{0:T(128)S(1)}, s32[6]{0:T(128)}, u32[]{:S(2)}) copy-start(s32[6]{0:T(128)} %order.1) | copy-start | bytes 76
  36.7 6.4 %collective-permute-start.3 = (bf16[32,2304]{1,0:T(8,128)(2,1)S(1)}, bf16[32,2304]{1,0:T(8,128)(2,1)S(1)}, u32[]{:S(2)}, u32[]{:S(2)}) collective-permute-start(bf16[32,2304]{1,0:T(8,128)(2,1)S(1)} %get-tuple-element.27), channel_id=1, source_target_pairs={{4,0},{0,4},{5,1},{1,5},{6,2},{2,6},{7,3},{3,7},{12,8},{8,12},{13,... | collective-permute-start | bytes 442376 | tf_op jit(solution)/shard_map/ppermute | solution.py:279
  36.8 9.9 %collective-permute-start.4 = (bf16[32,2304]{1,0:T(8,128)(2,1)S(1)}, bf16[32,2304]{1,0:T(8,128)(2,1)S(1)}, u32[]{:S(2)}, u32[]{:S(2)}) collective-permute-start(bf16[32,2304]{1,0:T(8,128)(2,1)S(1)} %get-tuple-element.29), channel_id=1, source_target_pairs={{4,0},{0,4},{5,1},{1,5},{6,2},{2,6},{7,3},{3,7},{12,8},{8,12},{13,... | collective-permute-start | bytes 442376 | tf_op jit(solution)/shard_map/ppermute | solution.py:279
  39.1 14.7 %collective-permute-start.5 = (bf16[64,2304]{1,0:T(8,128)(2,1)S(1)}, bf16[64,2304]{1,0:T(8,128)(2,1)S(1)}, u32[]{:S(2)}, u32[]{:S(2)}) collective-permute-start(bf16[64,2304]{1,0:T(8,128)(2,1)S(1)} %finish.3.refs_0_), channel_id=1, source_target_pairs={{0,8},{8,16},{16,24},{1,9},{9,17},{17,25},{2,10},{10,18},{18,26},{... | collective-permute-start | bytes 884744 | tf_op jit(solution)/shard_map/ppermute | solution.py:292
  43.3 8.9 %collective-permute-start.6 = (bf16[32,2304]{1,0:T(8,128)(2,1)S(1)}, bf16[32,2304]{1,0:T(8,128)(2,1)S(1)}, u32[]{:S(2)}, u32[]{:S(2)}) collective-permute-start(bf16[32,2304]{1,0:T(8,128)(2,1)S(1)} %finish.4.refs_1_), channel_id=1, source_target_pairs={{0,8},{8,16},{16,24},{1,9},{9,17},{17,25},{2,10},{10,18},{18,26},{... | collective-permute-start | bytes 442376 | tf_op jit(solution)/shard_map/ppermute | solution.py:292
  46.9 6.8 %collective-permute-start.7 = (bf16[32,2304]{1,0:T(8,128)(2,1)S(1)}, bf16[32,2304]{1,0:T(8,128)(2,1)S(1)}, u32[]{:S(2)}, u32[]{:S(2)}) collective-permute-start(bf16[32,2304]{1,0:T(8,128)(2,1)S(1)} %finish.5.refs_2_), channel_id=1, source_target_pairs={{0,8},{8,16},{16,24},{1,9},{9,17},{17,25},{2,10},{10,18},{18,26},{... | collective-permute-start | bytes 442376 | tf_op jit(solution)/shard_map/ppermute | solution.py:292

commit v2 on v1

v2 whole, which is shorter than its diff:
```python
import functools

import jax
import jax.numpy as jnp
import numpy as np
from jax import lax
from jax.experimental import pallas as pl
from jax.experimental.pallas import tpu as pltpu
from jax.sharding import PartitionSpec as P

HEAD_WIDTH = 128
EPSILON = 1e-06
SOFT_CAP = 50.0
QUERY_SCALE = 144.0 ** (-0.5)

VMEM = pl.BlockSpec(memory_space=pltpu.VMEM)
SMEM = pl.BlockSpec(memory_space=pltpu.SMEM)
HBM = pl.BlockSpec(memory_space=pltpu.HBM)
F32 = jnp.float32
BF16 = jnp.bfloat16


N_HELD = 9


def vmem_out(shape, dtype=BF16):
    return pltpu.VMEM(shape, dtype)


def chunks_of(seq_len):
    half, quarter = seq_len // 2, seq_len // 4
    return tuple(
        (c, c + half, tuple((p, p + quarter) for p in range(c, c + half, quarter)))
        for c in range(0, seq_len, half)
    )


def rotary_tables(seq_len):
    half = HEAD_WIDTH // 2
    freq = np.float32(10000.0) ** (np.float32(-2.0) * np.arange(half, dtype=np.float32) / np.float32(HEAD_WIDTH))
    angle = np.arange(seq_len, dtype=np.float32)[:, None] * freq[None, :]
    cosine, sine = np.cos(angle), np.sin(angle)
    return (
        np.concatenate([cosine, cosine], 1).astype(np.float32),
        np.concatenate([-sine, sine], 1).astype(np.float32),
    )


def rotate(values, cosine, sine):
    return values * cosine + pltpu.roll(values, HEAD_WIDTH // 2, 1) * sine


def column_steps(width):
    step = next(s for s in (768, 512, 384, 256, 128, width) if width % s == 0)
    return [(c, step) for c in range(0, width, step)]


def attend(normed, first, length, cosine, sine, prev, wq, wk, wv, wo, ready, sinks, kv_sinks):
    rows = normed.shape[0]
    kv_cols = wk.shape[1]
    group = wq.shape[1] // kv_cols
    total = first + rows
    heads = [slice(c, c + HEAD_WIDTH) for c in range(0, kv_cols, HEAD_WIDTH)]
    dot = functools.partial(jnp.dot, preferred_element_type=F32)

    def padded(values):
        if rows >= 128:
            return values
        return jnp.concatenate([values, jnp.zeros((128 - rows, values.shape[1]), values.dtype)], 0)

    full = padded(normed)
    ready("k")
    keys = dot(full, wk[...])[:rows]
    ready("v")
    vals = dot(full, wv[...])[:rows].astype(BF16)
    ready("q")
    queries = dot(full, wq[...])[:rows]
    keys = [rotate(keys[:, h], cosine, sine).astype(BF16) for h in heads]
    if kv_sinks is not None:
        for h, key in zip(heads, keys):
            kv_sinks[0][:, h] = key
        kv_sinks[1][...] = vals
    vals = [vals[:, h] for h in heads]
    if prev is not None:
        keys = [jnp.concatenate([prev[0][:, h], key], 0) for h, key in zip(heads, keys)]
        vals = [jnp.concatenate([prev[1][:, h], val], 0) for h, val in zip(heads, vals)]
    vals = [jnp.concatenate([val, jnp.ones_like(val)], 1) for val in vals]
    stacked = []
    for g in range(len(heads)):
        parts = [slice(c, c + HEAD_WIDTH) for c in range(g * group * HEAD_WIDTH, (g + 1) * group * HEAD_WIDTH, HEAD_WIDTH)]
        stacked.append(jnp.concatenate([rotate(queries[:, p], cosine, sine) for p in parts], 0).astype(BF16))
    q_pos = lax.broadcasted_iota(jnp.int32, (rows, total), 0) + first
    k_pos = lax.broadcasted_iota(jnp.int32, (rows, total), 1)
    allowed = (k_pos <= q_pos) & (k_pos < length)
    allowed = jnp.concatenate([allowed] * group, 0)
    scores = [
        lax.dot_general(q, k, (((1,), (1,)), ((), ())), preferred_element_type=F32)
        for q, k in zip(stacked, keys)
    ]
    raised = [
        jnp.where(allowed, jnp.exp(SOFT_CAP * jnp.tanh(s * (QUERY_SCALE / SOFT_CAP))), 0.0).astype(BF16)
        for s in scores
    ]
    outs = [dot(r, v) for r, v in zip(raised, vals)]
    outs = [(o[:, :HEAD_WIDTH] / o[:, HEAD_WIDTH:]).astype(BF16) for o in outs]
    mixed = jnp.concatenate([o[j * rows : (j + 1) * rows] for o in outs for j in range(group)], 1)
    mixed = padded(mixed)
    ready("o")
    for c, step in column_steps(wo.shape[1]):
        part = dot(mixed, wo[:, c : c + step])[:rows].astype(BF16)
        for (a, b), sink in sinks:
            sink[:, c : c + step] = part[a - first : b - first]


def length_of(lengths, sequence):
    at = lax.broadcasted_iota(jnp.int32, lengths.shape, 1) == sequence
    return jnp.sum(jnp.where(at, lengths[...], 0), -1, keepdims=True)


def normalize(values, gain):
    return values * lax.rsqrt(jnp.mean(values * values, -1, keepdims=True) + EPSILON) * gain


def own_kernel(axis, spans, nx, *refs):
    xs, refs = refs[:nx], refs[nx:]
    held, refs = refs[:N_HELD], refs[N_HELD:]
    outs, refs = refs[: len(spans)], refs[len(spans) :]
    kept, sems = refs[:N_HELD], refs[N_HELD]
    copies = [pltpu.make_async_copy(s, t, sems.at[i]) for i, (s, t) in enumerate(zip(held, kept))]
    for copy in copies:
        copy.start()
    pre_gain, _, cosine, sine, lengths, wk, wv, wq, wo = kept
    for copy in copies[: N_HELD - 4]:
        copy.wait()
    waits = dict(zip("kvqo", copies[N_HELD - 4 :]))
    normed = jnp.concatenate([normalize(x[...].astype(F32), pre_gain[...]).astype(BF16) for x in xs], 0)
    length = length_of(lengths, lax.axis_index(axis))
    attend(
        normed, 0, length, cosine[...], sine[...], None, wq, wk, wv, wo,
        lambda name: waits[name].wait(), list(zip(spans, outs)), None,
    )


def peer_kernel(axis, distance, first, spans, keep, x, *refs):
    (pre_gain, _, cosine, sine, lengths, wk, wv, wq, wo), refs = refs[:N_HELD], refs[N_HELD:]
    prev = None
    if first:
        prev, refs = refs[:2], refs[2:]
    outs, refs = refs[: len(spans)], refs[len(spans) :]
    n = lengths.shape[1]
    length = length_of(lengths, lax.rem(lax.axis_index(axis) + (n - distance), n))
    normed = normalize(x[...].astype(F32), pre_gain[...]).astype(BF16)
    rows = slice(first, first + x.shape[0])
    attend(
        normed, first, length, cosine[rows, :], sine[rows, :], prev, wq, wk, wv, wo,
        lambda name: None, list(zip(spans, outs)), refs[:2] if keep else None,
    )


def finish_kernel(offset, *refs):
    own, x, gain = refs[:3]
    others, out = refs[3:-1], refs[-1]
    rows = own.shape[0]
    branch = own[...].astype(F32)
    for other in others:
        branch = branch + other[...].astype(F32)
    held = x[offset : offset + rows, :].astype(F32)
    out[...] = (held + normalize(branch, gain[...])).astype(BF16)


def store_kernel(spans, order, fresh_rows, *refs):
    pieces, out, fresh, chosen, sems = refs[: len(spans)], *refs[-4:]
    pick = pltpu.make_async_copy(order, chosen, sems.at[len(spans)])
    pick.start()
    copies = [
        pltpu.make_async_copy(p, out.at[0, 0, a:b], sems.at[i])
        for i, (p, (a, b)) in enumerate(zip(pieces, spans))
    ]
    for c in copies:
        c.start()
    pick.wait()
    enter = pltpu.make_async_copy(fresh_rows.at[chosen[0], 0], fresh, sems.at[len(spans)])
    enter.start()
    for c in copies:
        c.wait()
    enter.wait()


def advance_kernel(axis, spans, *refs):
    pieces, fresh, out, sems = refs[: len(spans)], *refs[-3:]
    first = lax.axis_index(axis) == 0

    @pl.when(first)
    def _():
        copy = pltpu.make_async_copy(fresh, out.at[0, 0], sems.at[0])
        copy.start()
        copy.wait()

    @pl.when(jnp.logical_not(first))
    def _():
        copies = [
            pltpu.make_async_copy(p, out.at[0, 0, a:b], sems.at[i])
            for i, (p, (a, b)) in enumerate(zip(pieces, spans))
        ]
        for c in copies:
            c.start()
        for c in copies:
            c.wait()


def split_kernel(spans, x, *refs):
    outs, sems = refs[:-1], refs[-1]
    copies = [
        pltpu.make_async_copy(x.at[0, 0, a:b], out, sems.at[i])
        for i, (out, (a, b)) in enumerate(zip(outs, spans))
    ]
    for c in copies:
        c.start()
    for c in copies:
        c.wait()


def call(kernel, name, out_shape, in_specs, out_specs, args, scratch=(), us=1.0, limit=16 << 20):
    args = [pltpu.with_memory_space_constraint(a, pltpu.HBM) if s is HBM else a for a, s in zip(args, in_specs)]
    return pl.pallas_call(
        kernel,
        out_shape=out_shape,
        in_specs=in_specs,
        out_specs=out_specs,
        scratch_shapes=list(scratch),
        name=name,
        cost_estimate=pl.CostEstimate(flops=int(us * 1e7), bytes_accessed=1024, transcendentals=0),
        compiler_params=pltpu.CompilerParams(vmem_limit_bytes=limit),
    )(*args)


def shards(
    incoming,
    fresh_rows,
    entry_order,
    flight_lengths,
    pre_gain,
    post_gain,
    w_query,
    key_weight,
    value_weight,
    w_out,
):
    seq_len, model = incoming.shape[2:]
    chunks = chunks_of(seq_len)
    spans = [span for _, _, inner in chunks for span in inner]
    n_tp = lax.axis_size("tp")
    n_section = lax.axis_size("section")
    kv_cols = key_weight.shape[2]
    cosine, sine = (jnp.asarray(t) for t in rotary_tables(seq_len))
    held = [pre_gain, post_gain, cosine, sine, flight_lengths, key_weight[0], value_weight[0], w_query[0], w_out[0]]
    dma = pltpu.SemaphoreType.DMA

    xs = call(
        functools.partial(split_kernel, [(a, b) for a, b, _ in chunks]), "split",
        [vmem_out((b - a, model)) for a, b, _ in chunks], [HBM], [VMEM] * len(chunks),
        [incoming], [dma((len(chunks),))],
    )
    ahead = {d: [(i, (i + d) % n_tp) for i in range(n_tp)] for d in range(1, n_tp)}
    arrived = {d: [lax.ppermute(x, "tp", ahead[d]) for x in xs] for d in ahead}

    own = call(
        functools.partial(own_kernel, "tp", spans, len(xs)), "own",
        [vmem_out((b - a, model)) for a, b in spans] + [vmem_out(h.shape, h.dtype) for h in held],
        [VMEM] * len(xs) + [HBM] * N_HELD, [VMEM] * (len(spans) + N_HELD),
        [*xs, *held], [dma((N_HELD,))], us=6.0,
    )
    own, held = own[: len(spans)], own[len(spans) :]

    back = {span: [] for span in spans}
    for d in ahead:
        kept = []
        for c, (first, last, inner) in enumerate(chunks):
            keep = c + 1 < len(chunks)
            shapes = [vmem_out((b - a, model)) for a, b in inner]
            shapes += [vmem_out((last - first, kv_cols))] * 2 if keep else []
            prev = [jnp.concatenate(k, 0) if len(k) > 1 else k[0] for k in zip(*kept)]
            done = call(
                functools.partial(peer_kernel, "tp", d, first, inner, keep), f"peer{c}",
                shapes, [VMEM] * (1 + N_HELD + len(prev)), [VMEM] * len(shapes),
                [arrived[d][c], *held, *prev], us=3.0,
            )
            kept.append(done[len(inner) :])
            for span, part in zip(inner, done):
                back[span].append(lax.ppermute(part, "tp", [(t, s) for s, t in ahead[d]]))

    produced, moved = [], []
    ring = [(i, (i + 1) % n_section) for i in range(n_section)]
    for c, (first, last, inner) in enumerate(chunks):
        for span in inner:
            piece = call(
                functools.partial(finish_kernel, span[0] - first), "finish",
                vmem_out((span[1] - span[0], model)), [VMEM] * (3 + len(back[span])), VMEM,
                [own[spans.index(span)], xs[c], held[1], *back[span]], us=0.3,
            )
            produced.append(piece)
            moved.append(lax.ppermute(piece, "section", ring))
    full = jax.ShapeDtypeStruct(incoming.shape, incoming.dtype)
    stored, fresh = call(
        functools.partial(store_kernel, spans), "store",
        [full, vmem_out((seq_len, model))], [HBM, HBM] + [VMEM] * len(spans), [HBM, VMEM],
        [entry_order, fresh_rows, *produced],
        [pltpu.SMEM(entry_order.shape, entry_order.dtype), dma((len(spans) + 1,))], us=1.5,
    )
    advanced = call(
        functools.partial(advance_kernel, "section", spans), "advance", full,
        [VMEM] * (len(spans) + 1), HBM, [*moved, fresh], [dma((len(spans),))],
    )
    return stored, advanced


def solution(mesh):
    in_specs = (
        P("section", ("dp", "tp"), None, None),
        P(None, ("dp", "tp"), None, None),
        P("dp"),
        P("section", "dp"),
        P("section", None),
        P("section", None),
        P("section", None, "tp"),
        P("section", None, "tp"),
        P("section", None, "tp"),
        P("section", "tp", None),
    )
    out_specs = (P("section", ("dp", "tp"), None, None), P("section", ("dp", "tp"), None, None))
    return jax.shard_map(shards, mesh=mesh, in_specs=in_specs, out_specs=out_specs, check_vma=False)
```

time: 55.1 us -> 40.4 us (0.73)
  local copies, waits for them, and re-layouts: 12.1 us -> 0 us
  waiting for transfers between devices: 2.28 us -> 8.49 us
  Pallas kernels: 21.7 us -> 15.8 us
  starting transfers between devices: 17.7 us -> 15.1 us
    unnamed x24 -> x0, local copies, waits for them, and re-layouts: 12.1 us -> none
    ppermute x8 -> x10, waiting for transfers between devices: 2.28 us -> 8.49 us  [the longest x4 4.81 us: shards(): moved.append(lax.ppermute(piece, 'section', ring))]
    pallas_call x10, Pallas kernels: 21.7 us -> 15.8 us  [call(): pl.pallas_call(kernel, out_shape=out_shape, in_specs=in_specs, out_specs=...]
    ppermute x8 -> x10, starting transfers between devices: 17.7 us -> 15.1 us  [the longest x4 7.67 us: shards(): moved.append(lax.ppermute(piece, 'section', ring))]
  transfers between devices with their start and end apart: 8 -> 10, of which waited for: 3 -> 6; matrix products, arithmetic and copies ran while one was open for 0% -> 0% of each run, Pallas kernels for 38% -> 35%
where the time goes in v2:
time: 40.4 us; the launch traced here: 40.2 us
  Pallas kernels  15.8 us (39%)
  starting transfers between devices  15.1 us (37%)
  waiting for transfers between devices  8.49 us (21%)
  between operations  0.72 us (2%)
    pallas_call x10, Pallas kernels, call(): pl.pallas_call(kernel, out_shape=out_shape, in_specs=in_specs, out_specs=...  15.8 us
    ppermute x4, starting transfers between devices, shards(): moved.append(lax.ppermute(piece, 'section', ring))  7.67 us
    ppermute x4, waiting for transfers between devices, shards(): moved.append(lax.ppermute(piece, 'section', ring))  4.81 us
    ppermute x4, starting transfers between devices, shards(): back[span].append(lax.ppermute(part, 'tp', [(t, s) for s, t in ahead[d]]))  4.33 us
    ppermute x2, starting transfers between devices, shards(): arrived = {d: [lax.ppermute(x, 'tp', ahead[d]) for x in xs] for d in ahead}  3.14 us
    ppermute x2, waiting for transfers between devices, shards(): arrived = {d: [lax.ppermute(x, 'tp', ahead[d]) for x in xs] for d in ahead}  3.07 us
  transfers between devices with their start and end apart: 10, of which 6 were waited for; matrix products, arithmetic and copies ran while one was open for 0% of the time, Pallas kernels for 35%

profile of v2, /device:TPU:0, one launch (start us, length us, event | category | flops | bytes accessed | tf_op | source)
XLA Modules:
  0.0 40.2 jit_solution(8285135418068331789)
XLA Ops:
  0.6 1.1 %split.1 = (bf16[64,2304]{1,0:T(8,128)(2,1)S(1)}, bf16[64,2304]{1,0:T(8,128)(2,1)S(1)}) custom-call(bf16[1,1,128,2304]{3,2,1,0:T(8,128)(2,1)} %x.1), custom_call_target="tpu_custom_call" | custom-call | flops 10000000 | bytes 1024 | tf_op jit(solution)/shard_map/split/pallas_call | solution.py:225
  1.7 3.1 %collective-permute-start = (bf16[64,2304]{1,0:T(8,128)(2,1)S(1)}, bf16[64,2304]{1,0:T(8,128)(2,1)S(1)}, u32[]{:S(2)}, u32[]{:S(2)}) collective-permute-start(bf16[64,2304]{1,0:T(8,128)(2,1)S(1)} %get-tuple-element.25.refs_0_.refs_1_), channel_id=1, source_target_pairs={{0,4},{4,0},{1,5},{5,1},{2,6},{6,2},{3,7},{7,3},{8,12},{12,8},{9,1... | collective-permute-start | bytes 884744 | tf_op jit(solution)/shard_map/ppermute | solution.py:265
  4.8 0.1 collective-permute-start.3
  4.8 6.2 %own.1 = (bf16[32,2304]{1,0:T(8,128)(2,1)S(1)}, bf16[32,2304]{1,0:T(8,128)(2,1)S(1)}, bf16[32,2304]{1,0:T(8,128)(2,1)S(1)}, bf16[32,2304]{1,0:T(8,128)(2,1)S(1)}...) custom-call(bf16[64,2304]{1,0:T(8,128)(2,1)S(1)} %get-tuple-element., ...), custom_call_target="tpu_custom_call" | custom-call | flops 60000000 | bytes 1024 | tf_op jit(solution)/shard_map/own/pallas_call | solution.py:225
  11.0 1.6 %collective-permute-done.x = bf16[64,2304]{1,0:T(8,128)(2,1)S(1)} collective-permute-done((bf16[64,2304]{1,0:T(8,128)(2,1)S(1)}, bf16[64,2304]{1,0:T(8,128)(2,1)S(1)}, u32[]{:S(2)}, u32[]{:S(2)}) %collective-permute-start) | collective-permute-done | bytes 294944 | tf_op jit(solution)/shard_map/ppermute | solution.py:265
  12.6 2.7 %peer0.1 = (bf16[32,2304]{1,0:T(8,128)(2,1)S(1)}, bf16[32,2304]{1,0:T(8,128)(2,1)S(1)}, bf16[64,512]{1,0:T(8,128)(2,1)S(1)}, bf16[64,512]{1,0:T(8,128)(2,1)S(1)}) custom-call(bf16[64,2304]{1,0:T(8,128)(2,1)S(1)} %collective-permute-done.x, f32[1,2304]{1,0:T(1,128)S(1)} %get-tuple-element.29.refs_0_, f32[1,2304]{1,0:T(1,128)S(1)} %get-tuple-element.28.refs_1_.refs_2_, ...), custom_call_target="tpu_custom_call" | custom-call | flops 30000000 | bytes 1024 | tf_op jit(solution)/shard_map/peer0/pallas_call | solution.py:225
  15.3 2.1 %collective-permute-start.1 = (bf16[32,2304]{1,0:T(8,128)(2,1)S(1)}, bf16[32,2304]{1,0:T(8,128)(2,1)S(1)}, u32[]{:S(2)}, u32[]{:S(2)}) collective-permute-start(bf16[32,2304]{1,0:T(8,128)(2,1)S(1)} %get-tuple-element.37), channel_id=1, source_target_pairs={{4,0},{0,4},{5,1},{1,5},{6,2},{2,6},{7,3},{3,7},{12,8},{8,12},{13,... | collective-permute-start | bytes 442376 | tf_op jit(solution)/shard_map/ppermute | solution.py:290
  17.4 0.1 collective-permute-start.2
  17.5 1.5 %collective-permute-done.3.x = bf16[64,2304]{1,0:T(8,128)(2,1)S(1)} collective-permute-done((bf16[64,2304]{1,0:T(8,128)(2,1)S(1)}, bf16[64,2304]{1,0:T(8,128)(2,1)S(1)}, u32[]{:S(2)}, u32[]{:S(2)}) %collective-permute-start.3) | collective-permute-done | bytes 294944 | tf_op jit(solution)/shard_map/ppermute | solution.py:265
  18.9 2.7 %peer1.1 = (bf16[32,2304]{1,0:T(8,128)(2,1)S(1)}, bf16[32,2304]{1,0:T(8,128)(2,1)S(1)}) custom-call(bf16[64,2304]{1,0:T(8,128)(2,1)S(1)} %collective-permute-done.3.x, f32[1,2304]{1,0:T(1,128)S(1)} %get-tuple-element.29.refs_0_, f32[1,2304]{1,0:T(1,128)S(1)} %get-tuple-element.28.refs_1_.refs_2_, f32[128,128]{1,0:T(8,128)S(1)} %get-tuple-element.30.refs_2_, ...), custom_call_target="tpu_custom_call" | custom-call | flops 30000000 | bytes 1024 | tf_op jit(solution)/shard_map/peer1/pallas_call | solution.py:225
  21.6 2.1 %collective-permute-start.4 = (bf16[32,2304]{1,0:T(8,128)(2,1)S(1)}, bf16[32,2304]{1,0:T(8,128)(2,1)S(1)}, u32[]{:S(2)}, u32[]{:S(2)}) collective-permute-start(bf16[32,2304]{1,0:T(8,128)(2,1)S(1)} %get-tuple-element.43), channel_id=1, source_target_pairs={{4,0},{0,4},{5,1},{1,5},{6,2},{2,6},{7,3},{3,7},{12,8},{8,12},{13,... | collective-permute-start | bytes 442376 | tf_op jit(solution)/shard_map/ppermute | solution.py:290
  23.8 0.2 finish.4.refs_0_
  24.0 2.1 %collective-permute-start.6 = (bf16[32,2304]{1,0:T(8,128)(2,1)S(1)}, bf16[32,2304]{1,0:T(8,128)(2,1)S(1)}, u32[]{:S(2)}, u32[]{:S(2)}) collective-permute-start(bf16[32,2304]{1,0:T(8,128)(2,1)S(1)} %finish.4.refs_0_), channel_id=1, source_target_pairs={{0,8},{8,16},{16,24},{24,0},{1,9},{9,17},{17,25},{25,1},{2,10},{10... | collective-permute-start | bytes 442376 | tf_op jit(solution)/shard_map/ppermute | solution.py:302
  26.0 0.2 finish.5.refs_1_
  26.2 1.6 %collective-permute-start.7 = (bf16[32,2304]{1,0:T(8,128)(2,1)S(1)}, bf16[32,2304]{1,0:T(8,128)(2,1)S(1)}, u32[]{:S(2)}, u32[]{:S(2)}) collective-permute-start(bf16[32,2304]{1,0:T(8,128)(2,1)S(1)} %finish.5.refs_1_), channel_id=1, source_target_pairs={{0,8},{8,16},{16,24},{24,0},{1,9},{9,17},{17,25},{25,1},{2,10},{10... | collective-permute-start | bytes 442376 | tf_op jit(solution)/shard_map/ppermute | solution.py:302
  27.8 0.6 %collective-permute-done.4.refs_3_ = bf16[32,2304]{1,0:T(8,128)(2,1)S(1)} collective-permute-done((bf16[32,2304]{1,0:T(8,128)(2,1)S(1)}, bf16[32,2304]{1,0:T(8,128)(2,1)S(1)}, u32[]{:S(2)}, u32[]{:S(2)}) %collective-permute-start.4) | collective-permute-done | bytes 147488 | tf_op jit(solution)/shard_map/ppermute | solution.py:290
  28.4 0.2 finish.6.refs_2_
  28.6 2.1 %collective-permute-start.8 = (bf16[32,2304]{1,0:T(8,128)(2,1)S(1)}, bf16[32,2304]{1,0:T(8,128)(2,1)S(1)}, u32[]{:S(2)}, u32[]{:S(2)}) collective-permute-start(bf16[32,2304]{1,0:T(8,128)(2,1)S(1)} %finish.6.refs_2_), channel_id=1, source_target_pairs={{0,8},{8,16},{16,24},{24,0},{1,9},{9,17},{17,25},{25,1},{2,10},{10... | collective-permute-start | bytes 442376 | tf_op jit(solution)/shard_map/ppermute | solution.py:302
  30.7 0.2 finish.7.refs_3_
  30.9 1.8 %collective-permute-start.9 = (bf16[32,2304]{1,0:T(8,128)(2,1)S(1)}, bf16[32,2304]{1,0:T(8,128)(2,1)S(1)}, u32[]{:S(2)}, u32[]{:S(2)}) collective-permute-start(bf16[32,2304]{1,0:T(8,128)(2,1)S(1)} %finish.7.refs_3_), channel_id=1, source_target_pairs={{0,8},{8,16},{16,24},{24,0},{1,9},{9,17},{17,25},{25,1},{2,10},{10... | collective-permute-start | bytes 442376 | tf_op jit(solution)/shard_map/ppermute | solution.py:302
  32.7 1.8 %store.1 = (bf16[1,1,128,2304]{3,2,1,0:T(8,128)(2,1)}, bf16[128,2304]{1,0:T(8,128)(2,1)S(1)}) custom-call(s32[6]{0:T(128)} %order.1, bf16[6,1,128,2304]{3,2,1,0:T(8,128)(2,1)} %fresh_rows.1, bf16[32,2304]{1,0:T(8,128)(2,1)S(1)} %finish.4.refs_0_, bf16[32,2304]{1,0:T(8,128)(2,1)S(1)} %finish.5.refs_1_, bf16[32,2304]{1,0:T(8,128)(2,1)S(1)} %finish.6.refs_2_, ...), custom_call_target="tpu_custom_call" | custom-call | flops 15000000 | bytes 1024 | tf_op jit(solution)/shard_map/store/pallas_call | solution.py:225
  34.6 3.2 %collective-permute-done.8.refs_2_ = bf16[32,2304]{1,0:T(8,128)(2,1)S(1)} collective-permute-done((bf16[32,2304]{1,0:T(8,128)(2,1)S(1)}, bf16[32,2304]{1,0:T(8,128)(2,1)S(1)}, u32[]{:S(2)}, u32[]{:S(2)}) %collective-permute-start.8) | collective-permute-done | bytes 147488 | tf_op jit(solution)/shard_map/ppermute | solution.py:302
  37.8 1.6 %collective-permute-done.9.refs_3_ = bf16[32,2304]{1,0:T(8,128)(2,1)S(1)} collective-permute-done((bf16[32,2304]{1,0:T(8,128)(2,1)S(1)}, bf16[32,2304]{1,0:T(8,128)(2,1)S(1)}, u32[]{:S(2)}, u32[]{:S(2)}) %collective-permute-start.9) | collective-permute-done | bytes 147488 | tf_op jit(solution)/shard_map/ppermute | solution.py:302
  39.3 0.8 %advance.1 = bf16[1,1,128,2304]{3,2,1,0:T(8,128)(2,1)} custom-call(bf16[32,2304]{1,0:T(8,128)(2,1)S(1)} %collective-permute-done.6.refs_0_, bf16[32,2304]{1,0:T(8,128)(2,1)S(1)} %collective-permute-done.7.refs_1_, bf16[32,2304]{1,0:T(8,128)(2,1)S(1)} %collective-permute-done.8.refs_2_, bf16[32,2304]{1,0:T(8,128)(2,1)S(1)} %collective-permute-done.9.refs_3_, ...), custom_call_target="tpu_custom_call" | custom-call | flops 10000000 | bytes 1024 | tf_op jit(solution)/shard_map/advance/pallas_call | solution.py:225
  (6 shorter events, 0.2 us)
Async XLA Ops:
  1.7 10.9 %collective-permute-start = (bf16[64,2304]{1,0:T(8,128)(2,1)S(1)}, bf16[64,2304]{1,0:T(8,128)(2,1)S(1)}, u32[]{:S(2)}, u32[]{:S(2)}) collective-permute-start(bf16[64,2304]{1,0:T(8,128)(2,1)S(1)} %get-tuple-element.25.refs_0_.refs_1_), channel_id=1, source_target_pairs={{0,4},{4,0},{1,5},{5,1},{2,6},{6,2},{3,7},{7,3},{8,12},{12,8},{9,1... | collective-permute-start | bytes 884744 | tf_op jit(solution)/shard_map/ppermute | solution.py:265
  4.8 14.2 %collective-permute-start.3 = (bf16[64,2304]{1,0:T(8,128)(2,1)S(1)}, bf16[64,2304]{1,0:T(8,128)(2,1)S(1)}, u32[]{:S(2)}, u32[]{:S(2)}) collective-permute-start(bf16[64,2304]{1,0:T(8,128)(2,1)S(1)} %get-tuple-element.26.refs_1_), channel_id=1, source_target_pairs={{0,4},{4,0},{1,5},{5,1},{2,6},{6,2},{3,7},{7,3},{8,12},{12,8},{9,1... | collective-permute-start | bytes 884744 | tf_op jit(solution)/shard_map/ppermute | solution.py:265
  15.3 8.5 %collective-permute-start.1 = (bf16[32,2304]{1,0:T(8,128)(2,1)S(1)}, bf16[32,2304]{1,0:T(8,128)(2,1)S(1)}, u32[]{:S(2)}, u32[]{:S(2)}) collective-permute-start(bf16[32,2304]{1,0:T(8,128)(2,1)S(1)} %get-tuple-element.37), channel_id=1, source_target_pairs={{4,0},{0,4},{5,1},{1,5},{6,2},{2,6},{7,3},{3,7},{12,8},{8,12},{13,... | collective-permute-start | bytes 442376 | tf_op jit(solution)/shard_map/ppermute | solution.py:290
  17.4 8.6 %collective-permute-start.2 = (bf16[32,2304]{1,0:T(8,128)(2,1)S(1)}, bf16[32,2304]{1,0:T(8,128)(2,1)S(1)}, u32[]{:S(2)}, u32[]{:S(2)}) collective-permute-start(bf16[32,2304]{1,0:T(8,128)(2,1)S(1)} %get-tuple-element.39), channel_id=1, source_target_pairs={{4,0},{0,4},{5,1},{1,5},{6,2},{2,6},{7,3},{3,7},{12,8},{8,12},{13,... | collective-permute-start | bytes 442376 | tf_op jit(solution)/shard_map/ppermute | solution.py:290
  21.6 6.8 %collective-permute-start.4 = (bf16[32,2304]{1,0:T(8,128)(2,1)S(1)}, bf16[32,2304]{1,0:T(8,128)(2,1)S(1)}, u32[]{:S(2)}, u32[]{:S(2)}) collective-permute-start(bf16[32,2304]{1,0:T(8,128)(2,1)S(1)} %get-tuple-element.43), channel_id=1, source_target_pairs={{4,0},{0,4},{5,1},{1,5},{6,2},{2,6},{7,3},{3,7},{12,8},{8,12},{13,... | collective-permute-start | bytes 442376 | tf_op jit(solution)/shard_map/ppermute | solution.py:290
  23.7 7.0 %collective-permute-start.5 = (bf16[32,2304]{1,0:T(8,128)(2,1)S(1)}, bf16[32,2304]{1,0:T(8,128)(2,1)S(1)}, u32[]{:S(2)}, u32[]{:S(2)}) collective-permute-start(bf16[32,2304]{1,0:T(8,128)(2,1)S(1)} %get-tuple-element.45), channel_id=1, source_target_pairs={{4,0},{0,4},{5,1},{1,5},{6,2},{2,6},{7,3},{3,7},{12,8},{8,12},{13,... | collective-permute-start | bytes 442376 | tf_op jit(solution)/shard_map/ppermute | solution.py:290
  24.0 10.6 %collective-permute-start.6 = (bf16[32,2304]{1,0:T(8,128)(2,1)S(1)}, bf16[32,2304]{1,0:T(8,128)(2,1)S(1)}, u32[]{:S(2)}, u32[]{:S(2)}) collective-permute-start(bf16[32,2304]{1,0:T(8,128)(2,1)S(1)} %finish.4.refs_0_), channel_id=1, source_target_pairs={{0,8},{8,16},{16,24},{24,0},{1,9},{9,17},{17,25},{25,1},{2,10},{10... | collective-permute-start | bytes 442376 | tf_op jit(solution)/shard_map/ppermute | solution.py:302
  26.2 8.4 %collective-permute-start.7 = (bf16[32,2304]{1,0:T(8,128)(2,1)S(1)}, bf16[32,2304]{1,0:T(8,128)(2,1)S(1)}, u32[]{:S(2)}, u32[]{:S(2)}) collective-permute-start(bf16[32,2304]{1,0:T(8,128)(2,1)S(1)} %finish.5.refs_1_), channel_id=1, source_target_pairs={{0,8},{8,16},{16,24},{24,0},{1,9},{9,17},{17,25},{25,1},{2,10},{10... | collective-permute-start | bytes 442376 | tf_op jit(solution)/shard_map/ppermute | solution.py:302
  28.6 9.2 %collective-permute-start.8 = (bf16[32,2304]{1,0:T(8,128)(2,1)S(1)}, bf16[32,2304]{1,0:T(8,128)(2,1)S(1)}, u32[]{:S(2)}, u32[]{:S(2)}) collective-permute-start(bf16[32,2304]{1,0:T(8,128)(2,1)S(1)} %finish.6.refs_2_), channel_id=1, source_target_pairs={{0,8},{8,16},{16,24},{24,0},{1,9},{9,17},{17,25},{25,1},{2,10},{10... | collective-permute-start | bytes 442376 | tf_op jit(solution)/shard_map/ppermute | solution.py:302
  30.9 8.4 %collective-permute-start.9 = (bf16[32,2304]{1,0:T(8,128)(2,1)S(1)}, bf16[32,2304]{1,0:T(8,128)(2,1)S(1)}, u32[]{:S(2)}, u32[]{:S(2)}) collective-permute-start(bf16[32,2304]{1,0:T(8,128)(2,1)S(1)} %finish.7.refs_3_), channel_id=1, source_target_pairs={{0,8},{8,16},{16,24},{24,0},{1,9},{9,17},{17,25},{25,1},{2,10},{10... | collective-permute-start | bytes 442376 | tf_op jit(solution)/shard_map/ppermute | solution.py:302
